TPU v7x, 32 devices: a whole 2x2x4 slice. The times are simulated.
32 devices in a mesh: dp: 32 (over z, y, x, core).
Axes of the slice: x: 2, y: 2, z: 4, core: 2. Of those that a mesh axis runs over, the one named last changes fastest.
Arguments:
- features: bfloat16 [256, 128, 1024], P('dp'), may hold values from -16 to 16
- ln_gain: float32 [1024], replicated, may hold values from 0.5 to 1.5
- w_query: bfloat16 [1024, 1024], replicated, may hold values from -0.1875 to 0.1875
- w_key: bfloat16 [1024, 1024], replicated, may hold values from -0.1875 to 0.1875
- w_value: bfloat16 [1024, 1024], replicated, may hold values from -0.1875 to 0.1875
- w_out: bfloat16 [1024, 1024], replicated, may hold values from -0.1875 to 0.1875
- text_raw: bfloat16 [256, 1024], P('dp'), may hold values from -0.35 to 0.35
Outputs:
- loss: float32 [], replicated
- text_grad: float32 [256, 1024], P('dp')
- w_out_grad: bfloat16 [1024, 1024], replicated
All inputs are finite; a program needn't handle non-finite values.
Results may differ from a plain program's by a relative error of at most 0.009.
Values may be sent and summed in bfloat16 or wider, within the bound.
No kernel may reach another device: no remote copies, remote signals or barrier semaphores. Data moves between devices by JAX's collectives and lax.ppermute only.
A program may use at most 128 MiB of HBM per device.

v0:
```python
import jax
import jax.numpy as jnp
from jax import lax
from jax.sharding import PartitionSpec as P

HEADS = 16
inv_temp = 1.0 / 0.07
attn_temp = 8.0
epsilon = 1e-06


def layer_norm(inputs, gain):
    center = inputs - jnp.mean(inputs, axis=-1, keepdims=True)
    spread = jnp.mean(center * center, axis=-1, keepdims=True)
    return center * lax.rsqrt(spread + epsilon) * gain


def unit_heads(proj, heads):
    shaped = proj.reshape(proj.shape[0], proj.shape[1], heads, -1)
    return (shaped * lax.rsqrt(jnp.sum(shaped * shaped, axis=-1, keepdims=True) + epsilon)).astype(
        jnp.bfloat16
    )


def embed(feats, ln_gain, w_query, w_key, w_value, w_out):
    images, tokens, width = feats.shape
    inputs = feats.astype(jnp.float32)
    normed = layer_norm(inputs, ln_gain).astype(jnp.bfloat16).reshape(images * tokens, width)
    query = unit_heads(
        jnp.dot(normed, w_query, preferred_element_type=jnp.float32).reshape(images, tokens, width),
        HEADS,
    )
    key_heads = unit_heads(
        jnp.dot(normed, w_key, preferred_element_type=jnp.float32).reshape(images, tokens, width),
        HEADS,
    )
    value_heads = (
        jnp.dot(normed, w_value, preferred_element_type=jnp.float32)
        .reshape(images, tokens, HEADS, -1)
        .astype(jnp.bfloat16)
    )
    scores = attn_temp * jnp.einsum(
        "bqhd,bkhd->bhqk", query, key_heads, preferred_element_type=jnp.float32
    )
    expo = jnp.exp(scores)
    weights = (
        (expo / jnp.sum(expo, axis=-1, keepdims=True)).astype(jnp.bfloat16).astype(jnp.float32)
    )
    pooled = weights[:, :, 0, :] + jnp.mean(weights[:, :, 1:, :], axis=2)
    abar = jnp.einsum(
        "bhk,bkhd->bhd", pooled, value_heads.astype(jnp.float32), precision=lax.Precision.HIGHEST
    )
    abar = abar.reshape(images, width).astype(jnp.bfloat16)
    xbar = inputs[:, 0, :] + jnp.mean(inputs[:, 1:, :], axis=1)
    emb = xbar + jnp.dot(abar, w_out, preferred_element_type=jnp.float32)
    return (emb, abar)


def local(features, ln_gain, w_query, w_key, w_value, w_out, text_raw):
    images = features.shape[0]
    total = images * lax.axis_size("dp")
    offset = lax.axis_index("dp") * images
    text32 = text_raw.astype(jnp.float32)
    txt_norm = jnp.sqrt(jnp.sum(text32 * text32, axis=1, keepdims=True) + epsilon)
    txt_f = text32 / txt_norm
    txt_u = txt_f.astype(jnp.bfloat16)
    emb, abar = embed(features, ln_gain, w_query, w_key, w_value, w_out)
    emb_norm = jnp.sqrt(jnp.sum(emb * emb, axis=1, keepdims=True) + epsilon)
    img_f = emb / emb_norm
    img_u = img_f.astype(jnp.bfloat16)
    row_index = lax.broadcasted_iota(jnp.int32, (images, total), 0)
    col_index = lax.broadcasted_iota(jnp.int32, (images, total), 1)
    diag_mask = jnp.where(col_index == row_index + offset, 1.0, 0.0).astype(jnp.float32)
    all_img, all_txt = (
        lax.all_gather(img_u, "dp", axis=0, tiled=True),
        lax.all_gather(txt_u, "dp", axis=0, tiled=True),
    )
    logits = inv_temp * jnp.dot(all_img, all_txt.T, preferred_element_type=jnp.float32)
    exp_logits = jnp.exp(logits)
    rowsum = jnp.sum(exp_logits, axis=1)
    colsum = jnp.sum(exp_logits, axis=0)
    diag_logit = jnp.diagonal(logits)
    loss = (jnp.sum(jnp.log(rowsum) - diag_logit) + jnp.sum(jnp.log(colsum) - diag_logit)) / (
        2.0 * total
    )
    row_block = lax.dynamic_slice_in_dim(exp_logits, offset, images, 0)
    own_rowsum = lax.dynamic_slice_in_dim(rowsum, offset, images, 0)
    delta_rows = 0.5 * (row_block / own_rowsum[:, None] + row_block / colsum[None, :]) - diag_mask
    delta_rows = delta_rows.astype(jnp.bfloat16)
    col_block = lax.dynamic_slice_in_dim(exp_logits, offset, images, 1)
    own_colsum = lax.dynamic_slice_in_dim(colsum, offset, images, 0)
    delta_cols = 0.5 * (col_block / rowsum[:, None] + col_block / own_colsum[None, :]) - diag_mask.T
    delta_cols = delta_cols.astype(jnp.bfloat16)
    grad_img = inv_temp * jnp.dot(delta_rows, all_txt, preferred_element_type=jnp.float32)
    grad_txt = inv_temp * lax.dot_general(
        delta_cols, all_img, (((0,), (0,)), ((), ())), preferred_element_type=jnp.float32
    )
    text_grad = (grad_txt - txt_f * jnp.sum(txt_f * grad_txt, axis=1, keepdims=True)) / txt_norm
    emb_grad = (grad_img - img_f * jnp.sum(img_f * grad_img, axis=1, keepdims=True)) / emb_norm
    local_grad = jnp.dot(abar.astype(jnp.float32).T, emb_grad, precision=lax.Precision.HIGHEST)
    w_out_grad = lax.psum(local_grad, "dp").astype(jnp.bfloat16)
    return (loss, text_grad, w_out_grad)


def solution(mesh):
    placed = (P("dp", None, None), P(), P(), P(), P(), P(), P("dp", None))
    return jax.shard_map(
        local, mesh=mesh, in_specs=placed, out_specs=(P(), P("dp", None), P()), check_vma=False
    )
```

profile of v0, /device:TPU:0, one launch (start us, length us, event | category | flops | bytes accessed | tf_op | source)
XLA Modules:
  0.0 256.5 jit_solution(18150039622632288894)
XLA Ops:
  0.7 2.9 %convert_reduce_fusion = f32[8,128]{0,1:T(8,128)S(1)} fusion(bf16[8,128,1024]{2,1,0:T(8,128)(2,1)} %param.7), kind=kLoop, calls=%fused_computation.16 | loop fusion | flops 2096128 | bytes 2101248 | tf_op jit(solution)/shard_map/reduce_sum | solution.py:13
  3.6 2.9 %multiply_reduce_fusion.2 = f32[8,128]{0,1:T(8,128)S(1)} fusion(f32[8,128]{0,1:T(8,128)S(1)} %broadcast_multiply_fusion, bf16[8,128,1024]{2,1,0:T(8,128)(2,1)} %param.7), kind=kLoop, calls=%fused_computation.14 | loop fusion | flops 4193280 | bytes 2105344 | tf_op jit(solution)/shard_map/reduce_sum | solution.py:14
  6.5 2.7 %fusion.14 = bf16[8,128,1024,1]{2,0,1,3:T(8,128)(2,1)} fusion(f32[1024]{0:T(1024)S(1)} %copy-done.4, f32[8,128]{0,1:T(8,128)S(1)} %add_rsqrt_fusion.2, f32[8,128]{0,1:T(8,128)S(1)} %broadcast_multiply_fusion, bf16[8,128,1024]{2,1,0:T(8,128)(2,1)S(1)} %copy-done.1), kind=kLoop, calls=%fused_computation.32 | loop fusion | flops 5242880 | bytes 4206592 | tf_op jit(solution)/shard_map/convert_element_type | solution.py:28
  9.2 3.9 %copy.38 = bf16[1024,1024]{0,1:T(8,128)(2,1)} copy(bf16[1024,1024]{1,0:T(8,128)(2,1)} %param.10) | data formatting | bytes 4194304 | tf_op args[3]
  13.1 7.6 %multiply_reduce_fusion = (f32[8,128,16]{1,2,0:T(8,128)S(1)}, f32[8,128,16,64]{1,3,2,0:T(8,128)}) fusion(bf16[16,64,1024,1]{2,1,0,3:T(8,128)(2,1)} %bitcast.49, bf16[8,128,1024,1]{2,0,1,3:T(8,128)(2,1)} %fusion.14), kind=kOutput, calls=%fused_computation.10 | convolution fusion | flops 2149564416 | bytes 8454144 | tf_op jit(solution)/shard_map/dot_general | solution.py:34
  20.7 3.9 %copy.36 = bf16[1024,1024]{0,1:T(8,128)(2,1)} copy(bf16[1024,1024]{1,0:T(8,128)(2,1)} %param.9) | data formatting | bytes 4194304 | tf_op args[2]
  24.6 5.8 %multiply_reduce_fusion.1 = (f32[8,128,16]{1,2,0:T(8,128)S(1)}, f32[8,128,16,64]{1,3,2,0:T(8,128)S(1)}) fusion(bf16[16,64,1024,1]{2,1,0,3:T(8,128)(2,1)} %bitcast.48, bf16[8,128,1024,1]{2,0,1,3:T(8,128)(2,1)} %fusion.14), kind=kOutput, calls=%fused_computation.12 | convolution fusion | flops 2149564416 | bytes 8454144 | tf_op jit(solution)/shard_map/dot_general | solution.py:30
  30.4 1.3 fusion.6
  31.8 15.0 %fusion.5 = f32[8,16,128,128]{3,2,1,0:T(8,128)S(1)} fusion(f32[8,16,128,128]{3,2,1,0:T(8,128)S(1)} %fusion.6), kind=kOutput, calls=%fused_computation.17 | output fusion | flops 10502271 | bytes 16777216 | tf_op jit(solution)/shard_map/div | solution.py:47
  46.9 1.9 slice_reduce_fusion
  48.9 3.9 %copy.40 = bf16[1024,1024]{0,1:T(8,128)(2,1)} copy(bf16[1024,1024]{1,0:T(8,128)(2,1)} %param.11) | data formatting | bytes 4194304 | tf_op args[4]
  52.8 7.5 %convolution_convert_fusion = bf16[8,128,16,64]{3,0,2,1:T(8,128)(2,1)S(1)} fusion(bf16[16,64,1024,1]{2,1,0,3:T(8,128)(2,1)} %bitcast.50, f32[1024]{0:T(1024)S(1)} %copy-done.4, f32[8,128]{0,1:T(8,128)S(1)} %add_rsqrt_fusion.2, f32[8,128]{0,1:T(8,128)S(1)} %broadcast_multiply_fusion, bf16[8,128,1024]{2,1,0:T(8,128)(2,1)} %param.7), kind=kOutput, calls=%fused_computation.18 | convolution fusion | flops 2153775104 | bytes 6303744 | tf_op jit(solution)/shard_map/dot_general | solution.py:38
  60.3 7.0 %fusion.2 = f32[8,16,1,64]{3,2,1,0:T(1,128)S(1)} fusion(f32[8,16,128,1]{2,3,1,0:T(1,128)S(1)} %bitcast.51, bf16[8,128,16,64]{3,0,2,1:T(8,128)(2,1)S(1)} %convolution_convert_fusion), kind=kOutput, calls=%fused_computation.6 | convolution fusion | flops 12582912 | bytes 2195456 | tf_op jit(solution)/shard_map/bhk,bkhd->bhd/dot_general | solution.py:50
  67.4 2.8 %copy_convert_fusion = f32[8,128,1024]{2,0,1:T(8,128)S(1)} fusion(bf16[8,128,1024]{2,1,0:T(8,128)(2,1)} %param.7), kind=kLoop, calls=%fused_computation.27 | loop fusion | flops 1048576 | bytes 6291456 | tf_op jit(solution)/shard_map/convert_element_type | solution.py:27
  71.1 44.7 %all_gather.6 = bf16[256,1024]{1,0:T(8,128)(2,1)S(1)} all-gather(bf16[8,1024]{1,0:T(8,128)(2,1)S(1)} %fusion.45), channel_id=1, replica_groups=mesh['dp'=32] {'dp'}, dimensions={0}, use_global_device_ids=true | all-gather | bytes 540672 | tf_op jit(solution)/shard_map/all_gather | solution.py:75
  116.0 38.3 %all_gather.7 = bf16[256,1024]{1,0:T(8,128)(2,1)S(1)} all-gather(bf16[8,1024]{1,0:T(8,128)(2,1)S(1)} %fusion.44), channel_id=1, replica_groups=mesh['dp'=32] {'dp'}, dimensions={0}, use_global_device_ids=true | all-gather | bytes 540672 | tf_op jit(solution)/shard_map/all_gather | solution.py:76
  154.3 1.0 exponential_reduce_fusion
  155.4 1.3 multiply_reduce_fusion.3
  156.8 3.8 %fusion.23 = f32[1024,1024]{1,0:T(8,128)} fusion(bf16[8,1024]{1,0:T(8,128)(2,1)S(1)} %convert_element_type.55, f32[8,1024]{1,0:T(8,128)S(1)} %get-tuple-element.18, f32[8]{0:T(128)S(1)} %get-tuple-element.17, f32[8]{0:T(128)S(1)} %add_sqrt_fusion.1, f32[8,1024]{1,0:T(8,128)S(1)} %get-tuple-element.13), kind=kOutput, calls=%fused_computation.50 | convolution fusion | flops 100696064 | bytes 4276288 | tf_op jit(solution)/shard_map/dot_general | solution.py:100
  160.5 88.6 %all-reduce.1 = bf16[1024,1024]{1,0:T(8,128)(2,1)} all-reduce(f32[1024,1024]{1,0:T(8,128)} %fusion.23), channel_id=1, replica_groups=mesh['dp'=32] {'dp'}, use_global_device_ids=true, to_apply=%region_15.16 | all-reduce | flops 1048576 | bytes 6291456 | tf_op jit(solution)/shard_map/psum | solution.py:101
  249.2 1.0 multiply_reduce_fusion.4
  250.3 0.7 subtract_divide_fusion
  251.0 2.4 gather_fusion
  253.4 0.7 subtract_reduce_fusion
  (28 shorter events, 1.5 us)
Async XLA Ops:
  0.6 69.9 %copy-start = (bf16[1024,1024]{1,0:T(8,128)(2,1)S(1)}, bf16[1024,1024]{1,0:T(8,128)(2,1)}, u32[]{:S(2)}) copy-start(bf16[1024,1024]{1,0:T(8,128)(2,1)} %param.12) | copy-start | bytes 6291460
  0.6 5.8 %copy-start.1 = (bf16[8,128,1024]{2,1,0:T(8,128)(2,1)S(1)}, bf16[8,128,1024]{2,1,0:T(8,128)(2,1)}, u32[]{:S(2)}) copy-start(bf16[8,128,1024]{2,1,0:T(8,128)(2,1)} %param.7) | copy-start | bytes 6291460
  0.7 5.8 %copy-start.4 = (f32[1024]{0:T(1024)S(1)}, f32[1024]{0:T(1024)}, u32[]{:S(2)}) copy-start(f32[1024]{0:T(1024)} %param.8) | copy-start | bytes 12292
  24.6 5.8 %copy-start.2 = (f32[8,128,16,64]{1,3,2,0:T(8,128)S(1)}, f32[8,128,16,64]{1,3,2,0:T(8,128)}, u32[]{:S(2)}) copy-start(f32[8,128,16,64]{1,3,2,0:T(8,128)} %get-tuple-element.9) | copy-start | bytes 12582916
  70.2 45.6 %copy-start.3 = (bf16[8,1024]{1,0:T(8,128)(2,1)S(1)}, bf16[8,1024]{1,0:T(8,128)(2,1)}, u32[]{:S(2)}) copy-start(bf16[8,1024]{1,0:T(8,128)(2,1)} %param.13) | copy-start | bytes 49156
where the time goes:
time: 257 us
  blocking collectives  172 us (67%)
  matrix products  36.8 us (14%)
  other arithmetic  30.3 us (12%)
  local copies, waits for them, and re-layouts  14.5 us (6%)
  between operations  3.26 us (1%)
    psum x1, blocking collectives, local(): w_out_grad = lax.psum(local_grad, 'dp').astype(jnp.bfloat16)  88.6 us
    all_gather x1, blocking collectives, local(): lax.all_gather(img_u, 'dp', axis=0, tiled=True)  44.7 us
    all_gather x1, blocking collectives, local(): lax.all_gather(txt_u, 'dp', axis=0, tiled=True)  38.3 us
    div x1, other arithmetic, embed(): expo / jnp.sum(expo, axis=-1, keepdims=True)  15 us
    unnamed x13, local copies, waits for them, and re-layouts  11.8 us
    dot_general x1, matrix products, embed(): jnp.dot(normed, w_key, preferred_element_type=jnp.float32)  7.56 us
    dot_general x1, matrix products, embed(): jnp.dot(normed, w_value, preferred_element_type=jnp.float32)  7.53 us
    dot_general x1, matrix products, embed(): jnp.einsum('bhk,bkhd->bhd', pooled, value_heads.astype(jnp.float32), prec...  6.95 us

commit v1 on v0

--- a/solution.py
+++ b/solution.py
@@ -71,10 +71,14 @@
     row_index = lax.broadcasted_iota(jnp.int32, (images, total), 0)
     col_index = lax.broadcasted_iota(jnp.int32, (images, total), 1)
     diag_mask = jnp.where(col_index == row_index + offset, 1.0, 0.0).astype(jnp.float32)
-    all_img, all_txt = (
-        lax.all_gather(img_u, "dp", axis=0, tiled=True),
-        lax.all_gather(txt_u, "dp", axis=0, tiled=True),
-    )
+
+    def touch_halves(w_in, dev_axis):
+        return jnp.concatenate(
+            lax.all_to_all(jnp.stack(lax.axis_size(dev_axis) * [w_in], axis=0), dev_axis, 0, 0),
+            axis=0,
+        )
+
+    all_img, all_txt = (lax.all_gather(img_u, "dp", axis=0, tiled=True), touch_halves(txt_u, "dp"))
     logits = inv_temp * jnp.dot(all_img, all_txt.T, preferred_element_type=jnp.float32)
     exp_logits = jnp.exp(logits)
     rowsum = jnp.sum(exp_logits, axis=1)

time: 257 us -> 226 us (0.88)
  blocking collectives: 172 us -> 132 us
  starting transfers between devices: 0 us -> 7.33 us
    all_gather x1 -> x0, blocking collectives: 38.3 us -> none  [local(): lax.all_gather(txt_u, 'dp', axis=0, tiled=True)]
    all_to_all x0 -> x1, starting transfers between devices: none -> 7.33 us  [touch_halves(): lax.all_to_all(jnp.stack(lax.axis_size(dev_axis) * [w_in], axis=0), dev_a...]
    dot_general x1, matrix products: 7.56 us -> 3.49 us  [embed(): jnp.dot(normed, w_key, preferred_element_type=jnp.float32)]
    dot_general x1, matrix products: 6.95 us -> 10 us  [embed(): jnp.einsum('bhk,bkhd->bhd', pooled, value_heads.astype(jnp.float32), prec...]
    unnamed x13 -> x19, local copies, waits for them, and re-layouts: 11.8 us -> 12 us
  transfers between devices with their start and end apart: 0 -> 1, of which waited for: 0 -> 0; matrix products, arithmetic and copies ran while one was open for 0% -> 31% of each run, Pallas kernels for 0% -> 0%
where the time goes in v1:
time: 226 us; the launch traced here: 225 us
  blocking collectives  132 us (58%)
  matrix products  34.3 us (15%)
  other arithmetic  32.7 us (14%)
  local copies, waits for them, and re-layouts  15.6 us (7%)
  starting transfers between devices  7.33 us (3%)
  between operations  3.3 us (1%)
    psum x1, blocking collectives, local(): w_out_grad = lax.psum(local_grad, 'dp').astype(jnp.bfloat16)  88.3 us
    all_gather x1, blocking collectives, local(): lax.all_gather(img_u, 'dp', axis=0, tiled=True)  43.4 us
    div x1, other arithmetic, embed(): expo / jnp.sum(expo, axis=-1, keepdims=True)  15.3 us
    unnamed x19, local copies, waits for them, and re-layouts  12 us
    dot_general x1, matrix products, embed(): jnp.einsum('bhk,bkhd->bhd', pooled, value_heads.astype(jnp.float32), prec...  10 us
    dot_general x1, matrix products, embed(): jnp.dot(normed, w_value, preferred_element_type=jnp.float32)  9.04 us
    all_to_all x1, starting transfers between devices, touch_halves(): lax.all_to_all(jnp.stack(lax.axis_size(dev_axis) * [w_in], axis=0), dev_a...  7.33 us
  transfers between devices with their start and end apart: 1, of which 0 were waited for; matrix products, arithmetic and copies ran while one was open for 31% of the time, Pallas kernels for 0%

profile of v1, /device:TPU:0, one launch (start us, length us, event | category | flops | bytes accessed | tf_op | source)
XLA Modules:
  0.0 224.9 jit_solution(16333641841021918606)
XLA Ops:
  0.6 1.0 fusion.23
  1.6 0.8 fusion.46
  2.4 0.9 stack.2
  3.4 7.3 %all-to-all-start = ((bf16[32,8,1024]{2,1,0:T(8,128)(2,1)}), bf16[32,8,1024]{2,1,0:T(8,128)(2,1)S(1)}, u32[]{:S(2)}, u32[]{:S(2)}) async-start(bf16[32,8,1024]{2,1,0:T(8,128)(2,1)} %stack.2), calls=%async_computation | async-start | bytes 1048576 | tf_op jit(solution)/shard_map/all_to_all | solution.py:77
  10.7 2.8 %convert_reduce_fusion = f32[8,128]{0,1:T(8,128)S(1)} fusion(bf16[8,128,1024]{2,1,0:T(8,128)(2,1)} %param.7), kind=kLoop, calls=%fused_computation.16 | loop fusion | flops 2096128 | bytes 2101248 | tf_op jit(solution)/shard_map/reduce_sum | solution.py:13
  13.5 2.9 %multiply_reduce_fusion.2 = f32[8,128]{0,1:T(8,128)S(1)} fusion(f32[8,128]{0,1:T(8,128)S(1)} %broadcast_multiply_fusion, bf16[8,128,1024]{2,1,0:T(8,128)(2,1)} %param.7), kind=kLoop, calls=%fused_computation.14 | loop fusion | flops 4193280 | bytes 2105344 | tf_op jit(solution)/shard_map/reduce_sum | solution.py:14
  16.4 4.0 %copy.38 = bf16[1024,1024]{0,1:T(8,128)(2,1)} copy(bf16[1024,1024]{1,0:T(8,128)(2,1)} %param.10) | data formatting | bytes 4194304 | tf_op args[3]
  20.3 3.9 %copy.36 = bf16[1024,1024]{0,1:T(8,128)(2,1)} copy(bf16[1024,1024]{1,0:T(8,128)(2,1)} %param.9) | data formatting | bytes 4194304 | tf_op args[2]
  24.3 3.1 %fusion.14 = bf16[8,128,1024,1]{2,0,1,3:T(8,128)(2,1)S(1)} fusion(f32[1024]{0:T(1024)S(1)} %copy-done.7, f32[8,128]{0,1:T(8,128)S(1)} %add_rsqrt_fusion.2, f32[8,128]{0,1:T(8,128)S(1)} %broadcast_multiply_fusion, bf16[8,128,1024]{2,1,0:T(8,128)(2,1)} %param.7), kind=kLoop, calls=%fused_computation.32 | loop fusion | flops 5242880 | bytes 4206592 | tf_op jit(solution)/shard_map/convert_element_type | solution.py:28
  27.4 3.5 %multiply_reduce_fusion = (f32[8,128,16]{1,2,0:T(8,128)S(1)}, f32[8,128,16,64]{1,3,2,0:T(8,128)S(1)}) fusion(bf16[16,64,1024,1]{2,1,0,3:T(8,128)(2,1)S(1)} %bitcast.56, bf16[8,128,1024,1]{2,0,1,3:T(8,128)(2,1)S(1)} %fusion.14), kind=kOutput, calls=%fused_computation.10 | convolution fusion | flops 2149564416 | bytes 8454144 | tf_op jit(solution)/shard_map/dot_general | solution.py:34
  30.9 3.5 %multiply_reduce_fusion.1 = (f32[8,128,16]{1,2,0:T(8,128)S(1)}, f32[8,128,16,64]{1,3,2,0:T(8,128)S(1)}) fusion(bf16[16,64,1024,1]{2,1,0,3:T(8,128)(2,1)S(1)} %bitcast.55, bf16[8,128,1024,1]{2,0,1,3:T(8,128)(2,1)S(1)} %fusion.14), kind=kOutput, calls=%fused_computation.12 | convolution fusion | flops 2149564416 | bytes 8454144 | tf_op jit(solution)/shard_map/dot_general | solution.py:30
  34.4 1.3 fusion.6
  35.7 15.3 %fusion.5 = f32[8,16,128,128]{3,2,1,0:T(8,128)S(1)} fusion(f32[8,16,128,128]{3,2,1,0:T(8,128)S(1)} %fusion.6), kind=kOutput, calls=%fused_computation.17 | output fusion | flops 10502271 | bytes 16777216 | tf_op jit(solution)/shard_map/div | solution.py:47
  51.1 1.9 slice_reduce_fusion
  53.1 3.1 %copy_convert_fusion = f32[8,128,1024]{2,0,1:T(8,128)} fusion(bf16[8,128,1024]{2,1,0:T(8,128)(2,1)S(1)} %copy-done.1), kind=kLoop, calls=%fused_computation.27 | loop fusion | flops 1048576 | bytes 6291456 | tf_op jit(solution)/shard_map/convert_element_type | solution.py:27
  56.2 3.9 %copy.40 = bf16[1024,1024]{0,1:T(8,128)(2,1)} copy(bf16[1024,1024]{1,0:T(8,128)(2,1)} %param.11) | data formatting | bytes 4194304 | tf_op args[4]
  60.1 9.0 %convolution_convert_fusion = bf16[8,128,16,64]{3,0,2,1:T(8,128)(2,1)} fusion(bf16[16,64,1024,1]{2,1,0,3:T(8,128)(2,1)} %bitcast.57, f32[1024]{0:T(1024)S(1)} %copy-done.7, f32[8,128]{0,1:T(8,128)S(1)} %add_rsqrt_fusion.2, f32[8,128]{0,1:T(8,128)S(1)} %broadcast_multiply_fusion, bf16[8,128,1024]{2,1,0:T(8,128)(2,1)} %param.7), kind=kOutput, calls=%fused_computation.18 | convolution fusion | flops 2153775104 | bytes 6303744 | tf_op jit(solution)/shard_map/dot_general | solution.py:38
  69.5 10.0 %fusion.2 = f32[8,16,1,64]{3,2,1,0:T(1,128)S(1)} fusion(f32[8,16,128,1]{2,3,1,0:T(1,128)S(1)} %bitcast.58, bf16[8,128,16,64]{3,0,2,1:T(8,128)(2,1)} %convolution_convert_fusion), kind=kOutput, calls=%fused_computation.6 | convolution fusion | flops 12582912 | bytes 2195456 | tf_op jit(solution)/shard_map/bhk,bkhd->bhd/dot_general | solution.py:50
  79.7 1.3 multiply_reduce_fusion.5
  81.0 43.4 %all_gather.3 = bf16[256,1024]{1,0:T(8,128)(2,1)S(1)} all-gather(bf16[8,1024]{1,0:T(8,128)(2,1)S(1)} %fusion.47), channel_id=1, replica_groups=mesh['dp'=32] {'dp'}, dimensions={0}, use_global_device_ids=true | all-gather | bytes 540672 | tf_op jit(solution)/shard_map/all_gather | solution.py:81
  125.6 3.8 %fusion.25 = f32[1024,1024]{1,0:T(8,128)} fusion(bf16[8,1024]{1,0:T(8,128)(2,1)S(1)} %convert_element_type.55, f32[8,1024]{1,0:T(8,128)S(1)} %get-tuple-element.18, f32[8]{0:T(128)S(1)} %get-tuple-element.17, f32[8]{0:T(128)S(1)} %add_sqrt_fusion.1, f32[8,1024]{1,0:T(8,128)S(1)} %get-tuple-element.13), kind=kOutput, calls=%fused_computation.52 | convolution fusion | flops 100696064 | bytes 4276288 | tf_op jit(solution)/shard_map/dot_general | solution.py:104
  129.3 88.3 %all-reduce.1 = bf16[1024,1024]{1,0:T(8,128)(2,1)} all-reduce(f32[1024,1024]{1,0:T(8,128)} %fusion.25), channel_id=1, replica_groups=mesh['dp'=32] {'dp'}, use_global_device_ids=true, to_apply=%region_15.16 | all-reduce | flops 1048576 | bytes 6291456 | tf_op jit(solution)/shard_map/psum | solution.py:105
  217.6 1.0 multiply_reduce_fusion.4
  218.6 2.4 %gather_fusion = f32[256]{0:T(256)S(1)} fusion(f32[256,256]{0,1:T(8,128)S(1)} %get-tuple-element.14, s32[256]{0:T(256)S(1)} %bitcast.54), kind=kCustom, calls=%fused_computation | custom fusion | bytes 4096 | tf_op jit(solution)/shard_map/jit(diagonal)/cond/branch_0_fun/gather | solution.py:86
  (36 shorter events, 3.2 us)
Async XLA Ops:
  0.6 79.0 %copy-start = (bf16[1024,1024]{1,0:T(8,128)(2,1)S(1)}, bf16[1024,1024]{1,0:T(8,128)(2,1)}, u32[]{:S(2)}) copy-start(bf16[1024,1024]{1,0:T(8,128)(2,1)} %param.12) | copy-start | bytes 6291460
  3.4 121.1 %all-to-all-start = ((bf16[32,8,1024]{2,1,0:T(8,128)(2,1)}), bf16[32,8,1024]{2,1,0:T(8,128)(2,1)S(1)}, u32[]{:S(2)}, u32[]{:S(2)}) async-start(bf16[32,8,1024]{2,1,0:T(8,128)(2,1)} %stack.2), calls=%async_computation | async-start | bytes 1048576 | tf_op jit(solution)/shard_map/all_to_all | solution.py:77
  16.4 7.9 %copy-start.7 = (f32[1024]{0:T(1024)S(1)}, f32[1024]{0:T(1024)}, u32[]{:S(2)}) copy-start(f32[1024]{0:T(1024)} %param.8) | copy-start | bytes 12292
  24.3 3.1 %copy-start.4 = (bf16[1024,1024]{0,1:T(8,128)(2,1)S(1)}, bf16[1024,1024]{0,1:T(8,128)(2,1)}, u32[]{:S(2)}) copy-start(bf16[1024,1024]{0,1:T(8,128)(2,1)} %copy.38) | copy-start | bytes 6291460
  27.4 3.5 %copy-start.3 = (bf16[1024,1024]{0,1:T(8,128)(2,1)S(1)}, bf16[1024,1024]{0,1:T(8,128)(2,1)}, u32[]{:S(2)}) copy-start(bf16[1024,1024]{0,1:T(8,128)(2,1)} %copy.36) | copy-start | bytes 6291460
  51.1 2.0 copy-start.1
  60.1 9.0 %copy-start.2 = (f32[8,128,1024]{2,0,1:T(8,128)S(1)}, f32[8,128,1024]{2,0,1:T(8,128)}, u32[]{:S(2)}) copy-start(f32[8,128,1024]{2,0,1:T(8,128)} %copy_convert_fusion) | copy-start | bytes 12582916
  124.9 0.7 copy-start.5
  129.3 88.3 %copy-start.6 = (bf16[8,1024]{1,0:T(8,128)(2,1)S(1)}, bf16[8,1024]{1,0:T(8,128)(2,1)}, u32[]{:S(2)}) copy-start(bf16[8,1024]{1,0:T(8,128)(2,1)} %param.13) | copy-start | bytes 49156
